TPU v7x, 32 devices: a whole 2x2x4 slice. The times are simulated.
32 devices in a mesh: dp: 4 (over y, x), vocab: 8 (over z, core).
Axes of the slice: x: 2, y: 2, z: 4, core: 2. Of those that a mesh axis runs over, the one named last changes fastest.
Arguments:
- hidden: bfloat16 [1024, 8192], P('dp'), may hold values from -14 to 14
- weight: bfloat16 [8192, 8192], P('dp', 'vocab'), may hold values from -1 to 1, as said below
- targets: int32 [1024], P('dp'), may hold values from 0 to 8191
- cotangent: float32 [1024], P('dp'), may hold values from 1 to 8
Outputs:
- loss: float32 [1024], P('dp')
- grad_hidden: bfloat16 [1024, 8192], P('vocab', 'dp')
- grad_weight: bfloat16 [8192, 8192], P('dp', 'vocab')
Inputs may be any that keep to these rules, and one draw needn't show every extreme that they name: `weight`: entries drawn with standard deviation 4 / sqrt(8192).
All inputs are finite; a program needn't handle non-finite values.
Results may differ from a plain program's by a relative error of at most 0.0047.
Values may be sent and summed in bfloat16 or wider, within the bound.
No kernel may reach another device: no remote copies, remote signals or barrier semaphores. Data moves between devices by JAX's collectives and lax.ppermute only.
A program may use at most 128 MiB of HBM per device.

v0:
```python
import jax
import jax.numpy as jnp
from jax import lax
from jax.sharding import PartitionSpec as P


def shards(hidden, weight, targets, cotangent):
    vocab_width = weight.shape[1]
    spread = lax.all_to_all(hidden, "dp", split_axis=1, concat_axis=0, tiled=True)
    vocab_first = lax.axis_index("vocab") * vocab_width
    columns = vocab_first + lax.iota(jnp.int32, vocab_width)
    onehot = (targets[:, None] == columns[None, :]).astype(jnp.float32)
    row_block = spread
    logits = lax.psum_scatter(
        jnp.dot(row_block, weight, preferred_element_type=jnp.float32),
        "dp",
        scatter_dimension=0,
        tiled=True,
    )
    local_max = jnp.max(logits, axis=1)
    local_pick = jnp.sum(logits * onehot, axis=1)
    row_max = lax.pmax(local_max, "vocab")
    shifted = jnp.exp(logits - row_max[:, None])
    sum_exp, picked = lax.psum((jnp.sum(shifted, axis=1), local_pick), "vocab")
    loss = row_max + jnp.log(sum_exp) - picked
    grad_logits = (cotangent[:, None] * (shifted / sum_exp[:, None] - onehot)).astype(jnp.bfloat16)
    all_grads = lax.all_gather(grad_logits, "dp", axis=0, tiled=True)
    grad_weight = lax.dot_general(
        spread, all_grads, (((0,), (0,)), ((), ())), preferred_element_type=jnp.float32
    ).astype(jnp.bfloat16)
    row_block = all_grads
    grad_hidden = lax.psum_scatter(
        lax.dot_general(
            row_block, weight, (((1,), (1,)), ((), ())), preferred_element_type=jnp.float32
        ),
        "vocab",
        scatter_dimension=0,
        tiled=True,
    ).astype(jnp.bfloat16)
    return (loss, grad_hidden, grad_weight)


def solution(mesh):
    in_specs = (P("dp", None), P("dp", "vocab"), P("dp"), P("dp"))
    out_specs = (P("dp"), P("vocab", "dp"), P("dp", "vocab"))
    return jax.shard_map(shards, mesh=mesh, in_specs=in_specs, out_specs=out_specs, check_vma=False)
```

profile of v0, /device:TPU:0, one launch (start us, length us, event | category | flops | bytes accessed | tf_op | source)
XLA Modules:
  0.0 314.0 jit_solution(2251081179240819122)
XLA Ops:
  7.2 0.0 reduce-scatter.3.cloned.1.call-start
  7.2 6.4 %copy.9 = bf16[256,8192]{0,1:T(8,128)(2,1)} copy(bf16[256,8192]{1,0:T(8,128)(2,1)} %param.4) | data formatting | bytes 8388608 | tf_op args[0]
  13.6 55.1 %all_to_all.19 = bf16[256,4,2048]{0,2,1:T(8,128)(2,1)} all-to-all(bf16[256,4,2048]{0,2,1:T(8,128)(2,1)} %bitcast.12), channel_id=1, replica_groups=mesh['dp'=4,'vocab'=8] {'dp'}, dimensions={1} | all-to-all | bytes 8388608 | tf_op jit(solution)/shard_map/all_to_all | solution.py:9
  68.7 6.2 %copy.10 = bf16[4,256,2048]{2,1,0:T(8,128)(2,1)} copy(bf16[4,256,2048]{1,2,0:T(8,128)(2,1)} %bitcast.11) | data formatting | bytes 8388608 | tf_op jit(solution)/shard_map/all_to_all | solution.py:9
  74.9 9.9 %fusion.5 = f32[1024,1024]{1,0:T(8,128)} fusion(bf16[1024,2048]{1,0:T(8,128)(2,1)} %bitcast.13, bf16[2048,1024]{1,0:T(8,128)(2,1)} %param.5), kind=kOutput, calls=%fused_computation.11 | convolution fusion | flops 4294967296 | bytes 12582912 | tf_op jit(solution)/shard_map/dot_general | solution.py:15
  84.7 0.0 copy-start
  84.8 0.0 copy-start.1
  84.8 0.0 reduce-scatter.3.cloned.1.call-update
  84.8 0.0 all-gather.2.cloned.1.call-start
  84.8 52.6 %reduce-scatter.3.cloned.1.call-done = f32[256,1024]{1,0:T(8,128)} async-done(((f32[1024,1024]{1,0:T(8,128)}), f32[256,1024]{1,0:T(8,128)}) %reduce-scatter.3.cloned.1.call-update) | async-done | bytes 1048592 | tf_op jit(solution)/shard_map/reduce_scatter | solution.py:14
  137.4 1.4 reduce_max.9
  138.8 16.2 %pmax.7 = f32[256]{0:T(256)S(1)} all-reduce(f32[256]{0:T(256)S(1)} %reduce_max.9), channel_id=1, replica_groups=mesh['dp'=4,'vocab'=8] {'vocab'}, use_global_device_ids=true, to_apply=%region_2.0 | all-reduce | flops 256 | bytes 2048 | tf_op jit(solution)/shard_map/pmax | solution.py:22
  155.0 0.0 copy-done
  155.0 1.6 fusion.4
  156.6 13.6 %all-reduce = (f32[256]{0:T(256)S(1)}, f32[256]{0:T(256)S(1)}) all-reduce(f32[256]{0:T(256)S(1)} %get-tuple-element.13, f32[256]{0:T(256)S(1)} %get-tuple-element.12), channel_id=1, replica_groups=mesh['dp'=4,'vocab'=8] {'vocab'}, use_global_device_ids=true, to_apply=%region_6.0 | all-reduce | flops 512 | bytes 4096 | tf_op jit(solution)/shard_map/psum | solution.py:24
  170.2 0.0 copy-done.1
  170.2 2.4 fusion.3
  172.6 0.0 all-gather.2.cloned.1.call-update
  172.6 0.0 reduce-scatter.5.cloned.1.call-start
  172.6 32.5 %all-gather.2.cloned.1.call-done = bf16[1024,1024]{1,0:T(8,128)(2,1)} async-done(((bf16[256,1024]{1,0:T(8,128)(2,1)}), bf16[1024,1024]{1,0:T(8,128)(2,1)}) %all-gather.2.cloned.1.call-update) | async-done | bytes 2097168 | tf_op jit(solution)/shard_map/all_gather | solution.py:27
  205.1 10.6 %fusion.6 = f32[1024,2048]{1,0:T(8,128)} fusion(bf16[1024,1024]{1,0:T(8,128)(2,1)} %all-gather.2.cloned.1.call-done, bf16[2048,1024]{1,0:T(8,128)(2,1)} %param.5), kind=kOutput, calls=%fused_computation.12 | convolution fusion | flops 4294967296 | bytes 14680064 | tf_op jit(solution)/shard_map/dot_general | solution.py:33
  215.7 0.0 copy-start.2
  215.7 0.0 reduce-scatter.5.cloned.1.call-update
  215.7 0.6 add_subtract_fusion
  216.3 1.0 copy-done.2
  217.3 8.3 %convert_bitcast_fusion = bf16[2048,1024]{0,1:T(8,128)(2,1)} fusion(bf16[1024,1024]{1,0:T(8,128)(2,1)S(1)} %copy-done.2, bf16[1024,2048]{1,0:T(8,128)(2,1)} %bitcast.14), kind=kOutput, calls=%fused_computation | convolution fusion | flops 4297064448 | bytes 10485760 | tf_op jit(solution)/shard_map/dot_general | solution.py:28
  225.6 6.4 %copy.11 = bf16[2048,1024]{1,0:T(8,128)(2,1)} copy(bf16[2048,1024]{0,1:T(8,128)(2,1)} %convert_bitcast_fusion) | data formatting | bytes 8388608
  232.0 73.4 %reduce-scatter.5.cloned.1.call-done = f32[128,2048]{1,0:T(8,128)} async-done(((f32[1024,2048]{1,0:T(8,128)}), f32[128,2048]{1,0:T(8,128)}) %reduce-scatter.5.cloned.1.call-update) | async-done | bytes 1048592 | tf_op jit(solution)/shard_map/reduce_scatter | solution.py:32
  305.4 2.1 convert_element_type.17
  (1 shorter events, 0.0 us)
Async XLA Ops:
  7.2 130.3 %reduce-scatter.3.cloned.1.call-start = ((), (), s32[]{:S(2)}) async-start(), calls=%async_computation.3 | async-start | bytes 5242880 | tf_op jit(solution)/shard_map/reduce_scatter | solution.py:14
  84.7 70.2 %copy-start = (s32[256]{0:T(256)S(1)}, s32[256]{0:T(256)}, u32[]{:S(2)}) copy-start(s32[256]{0:T(256)} %param.6) | copy-start | bytes 3076
  84.8 85.4 %copy-start.1 = (f32[256]{0:T(256)S(1)}, f32[256]{0:T(256)}, u32[]{:S(2)}) copy-start(f32[256]{0:T(256)} %param.7) | copy-start | bytes 3076
  84.8 120.4 %all-gather.2.cloned.1.call-start = ((), (), s32[]{:S(2)}) async-start(), calls=%async_computation.4 | async-start | bytes 2621440 | tf_op jit(solution)/shard_map/all_gather | solution.py:27
  172.6 132.9 %reduce-scatter.5.cloned.1.call-start = ((), (), s32[]{:S(2)}) async-start(), calls=%async_computation.5 | async-start | bytes 9437184 | tf_op jit(solution)/shard_map/reduce_scatter | solution.py:32
  215.7 1.6 copy-start.2
Sparse Core Ops, SparseCore 0:
  84.9 52.4 reduce-scatter.2
  172.7 32.3 all-gather.1
  215.9 89.5 reduce-scatter.4
where the time goes:
time: 315 us; the launch traced here: 314 us
  waiting for transfers between devices  159 us (50%)
  blocking collectives  84.9 us (27%)
  matrix products  28.7 us (9%)
  local copies, waits for them, and re-layouts  20 us (6%)
  between operations  13.8 us (4%)
  other arithmetic  8 us (3%)
    reduce_scatter x1, waiting for transfers between devices, shards(): lax.psum_scatter(lax.dot_general(row_block, weight, (((1,), (1,)), ((), (...  73.4 us
    all_to_all x1, blocking collectives, shards(): lax.all_to_all(hidden, 'dp', split_axis=1, concat_axis=0, tiled=True)  55.1 us
    reduce_scatter x1, waiting for transfers between devices, shards(): lax.psum_scatter(jnp.dot(row_block, weight, preferred_element_type=jnp.fl...  52.6 us
    all_gather x1, waiting for transfers between devices, shards(): all_grads = lax.all_gather(grad_logits, 'dp', axis=0, tiled=True)  32.5 us
    pmax x1, blocking collectives, shards(): row_max = lax.pmax(local_max, 'vocab')  16.2 us
    unnamed x8, local copies, waits for them, and re-layouts  13.8 us
    psum x1, blocking collectives, shards(): sum_exp, picked = lax.psum((jnp.sum(shifted, axis=1), local_pick), 'vocab')  13.6 us
    dot_general x1, matrix products, shards(): lax.dot_general(row_block, weight, (((1,), (1,)), ((), ())), preferred_el...  10.6 us
  transfers between devices with their start and end apart: 3, of which 3 were waited for; matrix products, arithmetic and copies ran while one was open for 5% of the time, Pallas kernels for 0%

commit v1 on v0

v1 whole, which is shorter than its diff:
```python
import jax
import jax.numpy as jnp
from jax import lax
from jax.sharding import Mesh, PartitionSpec as P

CORES = 2


def forward_dot(rows, weight):
    return jnp.dot(rows, weight, preferred_element_type=jnp.float32)


def hidden_dot(grads, weight):
    return lax.dot_general(grads, weight, (((1,), (1,)), ((), ())), preferred_element_type=jnp.float32)


def shards(hidden, weight, targets, cotangent):
    dp, deep = lax.axis_size("dp"), lax.axis_size("z")
    own, vocab_width = hidden.shape[0], weight.shape[1]
    block = own * dp // (deep * CORES)
    core = lax.axis_index("core")
    swap = [(0, 1), (1, 0)]

    def halves(x):
        parts = x.reshape((own // (CORES * block), CORES, block) + x.shape[1:])
        pick = lambda c: lax.dynamic_index_in_dim(parts, c, 1, keepdims=False).reshape((own // CORES,) + x.shape[1:])
        return pick(core), pick(1 - core)

    mine = lax.all_to_all(halves(hidden)[0], "dp", split_axis=1, concat_axis=0, tiled=True)
    other = lax.ppermute(mine, "core", swap)
    half = mine.shape[0]

    def scatter(part):
        return lax.psum_scatter(part, "dp", scatter_dimension=0, tiled=True)

    both = jnp.concatenate([forward_dot(mine, weight).reshape(dp, 1, half // dp, vocab_width), forward_dot(other, weight).reshape(dp, 1, half // dp, vocab_width)], axis=1)
    logits = scatter(both.reshape(2 * half, vocab_width)).reshape(2, half // dp, vocab_width)
    goal = jnp.stack(halves(targets))
    cot = jnp.stack(halves(cotangent))
    first = (lax.axis_index("z") * CORES + core) * vocab_width
    onehot = (goal[:, :, None] == first + lax.iota(jnp.int32, vocab_width)).astype(jnp.float32)
    local_max = jnp.max(logits, axis=2)
    shifted = jnp.exp(logits - local_max[:, :, None])
    local = jnp.stack([local_max, jnp.sum(shifted, axis=2), jnp.sum(logits * onehot, axis=2)])
    order = jnp.where(core == 0, local, local[:, ::-1])
    every = lax.all_gather(order, ("z", "core"), axis=0)
    maxima = every[:, 0]
    row_max = jnp.max(maxima, axis=0)
    sum_exp = jnp.sum(every[:, 1] * jnp.exp(maxima - row_max), axis=0)
    loss = row_max + jnp.log(sum_exp) - jnp.sum(every[:, 2], axis=0)
    loss = loss.reshape(CORES, own // (CORES * block), block).swapaxes(0, 1).reshape(own)
    turn = lambda x: jnp.where(core == 0, x, x[::-1])
    row_max, sum_exp = turn(row_max), turn(sum_exp)
    scale = jnp.exp(local_max - row_max) / sum_exp
    grads = (cot[:, :, None] * (shifted * scale[:, :, None] - onehot)).astype(jnp.bfloat16)
    gathered = lax.all_gather(grads, "dp", axis=0, tiled=False)
    mine_grads = gathered[:, 0].reshape(half, vocab_width)
    other_grads = gathered[:, 1].reshape(half, vocab_width)
    away = lax.ppermute(hidden_dot(other_grads, weight).astype(jnp.bfloat16), "core", swap)
    part = hidden_dot(mine_grads, weight) + away.astype(jnp.float32)
    grad_hidden = lax.psum_scatter(part.astype(jnp.bfloat16), "z", scatter_dimension=0, tiled=True)
    weigh = lambda h, g: lax.dot_general(h, g, (((0,), (0,)), ((), ())), preferred_element_type=jnp.float32)
    rows = jnp.concatenate([mine, other])
    grad_weight = weigh(rows, jnp.concatenate([mine_grads, other_grads])).astype(jnp.bfloat16)
    return (loss, grad_hidden, grad_weight)


def solution(mesh):
    dp, vocab = mesh.shape["dp"], mesh.shape["vocab"]
    fine = Mesh(mesh.devices.reshape(dp, vocab // CORES, CORES), ("dp", "z", "core"))
    cols = ("z", "core")
    in_specs = (P("dp", None), P("dp", cols), P("dp"), P("dp"))
    out_specs = (P("dp"), P(cols, "dp"), P("dp", cols))
    return jax.shard_map(shards, mesh=fine, in_specs=in_specs, out_specs=out_specs, check_vma=False)
```

time: 315 us -> 228 us (0.72)
  blocking collectives: 84.9 us -> 44.9 us
  waiting for transfers between devices: 159 us -> 128 us
  matrix products: 28.7 us -> 19.2 us
  local copies, waits for them, and re-layouts: 20 us -> 14.7 us
    reduce_scatter x2, waiting for transfers between devices: 126 us -> 87.2 us  [the longest x1 51.9 us: scatter(): return lax.psum_scatter(part, 'dp', scatter_dimension=0, tiled=True)]
    all_to_all x1, blocking collectives: 55.1 us -> 30.8 us  [shards(): lax.all_to_all(halves(hidden)[0], 'dp', split_axis=1, concat_axis=0, tile...]
    pmax x1 -> x0, blocking collectives: 16.2 us -> none  [shards(): row_max = lax.pmax(local_max, 'vocab')]
    all_gather x0 -> x1, blocking collectives: none -> 14 us  [shards(): every = lax.all_gather(order, ('z', 'core'), axis=0)]
    psum x1 -> x0, blocking collectives: 13.6 us -> none  [shards(): sum_exp, picked = lax.psum((jnp.sum(shifted, axis=1), local_pick), 'vocab')]
    unnamed x8 -> x12, local copies, waits for them, and re-layouts: 13.8 us -> 1.55 us
    dot_general x3 -> x5, matrix products: 28.7 us -> 19.2 us  [the longest x1 8.44 us: shards(): lax.dot_general(h, g, (((0,), (0,)), ((), ())), preferred_element_type=jn...]
    dynamic_slice x0 -> x2, local copies, waits for them, and re-layouts: none -> 6.31 us  [halves(): lax.dynamic_index_in_dim(parts, c, 1, keepdims=False)]
  transfers between devices with their start and end apart: 3 -> 5, of which waited for: 3 -> 5; matrix products, arithmetic and copies ran while one was open for 5% -> 5% of each run, Pallas kernels for 0% -> 0%
where the time goes in v1:
time: 228 us
  waiting for transfers between devices  128 us (56%)
  blocking collectives  44.9 us (20%)
  matrix products  19.2 us (8%)
  local copies, waits for them, and re-layouts  14.7 us (6%)
  between operations  13.9 us (6%)
  other arithmetic  6.62 us (3%)
    reduce_scatter x1, waiting for transfers between devices, scatter(): return lax.psum_scatter(part, 'dp', scatter_dimension=0, tiled=True)  51.9 us
    reduce_scatter x1, waiting for transfers between devices, shards(): lax.psum_scatter(part.astype(jnp.bfloat16), 'z', scatter_dimension=0, til...  35.3 us
    all_gather x1, waiting for transfers between devices, shards(): gathered = lax.all_gather(grads, 'dp', axis=0, tiled=False)  34.9 us
    all_to_all x1, blocking collectives, shards(): lax.all_to_all(halves(hidden)[0], 'dp', split_axis=1, concat_axis=0, tile...  30.8 us
    all_gather x1, blocking collectives, shards(): every = lax.all_gather(order, ('z', 'core'), axis=0)  14 us
    dot_general x1, matrix products, shards(): lax.dot_general(h, g, (((0,), (0,)), ((), ())), preferred_element_type=jn...  8.44 us
    dynamic_slice x2, local copies, waits for them, and re-layouts, halves(): lax.dynamic_index_in_dim(parts, c, 1, keepdims=False)  6.31 us
    dot_general x2, matrix products, hidden_dot(): lax.dot_general(grads, weight, (((1,), (1,)), ((), ())), preferred_elemen...  6.06 us
  transfers between devices with their start and end apart: 5, of which 5 were waited for; matrix products, arithmetic and copies ran while one was open for 5% of the time, Pallas kernels for 0%

profile of v1, /device:TPU:0, one launch (start us, length us, event | category | flops | bytes accessed | tf_op | source)
XLA Modules:
  0.0 227.8 jit_solution(10791145434281866014)
XLA Ops:
  7.2 0.0 reduce-scatter.3.cloned.1.call-start
  7.2 3.1 %constant_dynamic-slice_fusion.4 = bf16[1,1,128,8192]{3,2,1,0:T(8,128)(2,1)} fusion(bf16[1,2,128,8192]{3,2,1,0:T(8,128)(2,1)} %bitcast.68, s32[]{:T(128)S(6)} %select_n.33), kind=kLoop, calls=%fused_computation.32 | loop fusion | bytes 4194308 | tf_op jit(solution)/shard_map/jit(dynamic_index_in_dim)/dynamic_slice | solution.py:26
  10.3 3.2 %copy.15 = bf16[1,1,128,8192]{2,3,1,0:T(8,128)(2,1)S(1)} copy(bf16[1,1,128,8192]{3,2,1,0:T(8,128)(2,1)} %constant_dynamic-slice_fusion.4) | data formatting | bytes 4194304 | tf_op jit(solution)/shard_map/jit(dynamic_index_in_dim)/dynamic_slice | solution.py:26
  13.5 2.6 %copy.16 = bf16[128,4,2048]{2,0,1:T(8,128)(2,1)} copy(bf16[128,4,2048]{0,2,1:T(8,128)(2,1)S(1)} %bitcast.64) | data formatting | bytes 4194304 | tf_op jit(solution)/shard_map/all_to_all | solution.py:29
  16.1 30.8 %all_to_all.19 = bf16[128,4,2048]{2,0,1:T(8,128)(2,1)S(1)} all-to-all(bf16[128,4,2048]{2,0,1:T(8,128)(2,1)} %copy.16), channel_id=1, replica_groups=mesh['dp'=4,'z'=4,'core'=2] {'dp'}, dimensions={1} | all-to-all | bytes 4194304 | tf_op jit(solution)/shard_map/all_to_all | solution.py:29
  47.0 2.4 %fusion.13 = f32[4,1,128,1024]{3,2,0,1:T(8,128)S(1)} fusion(bf16[2048,1024]{1,0:T(8,128)(2,1)S(1)} %copy-done.3, bf16[128,4,2048]{2,0,1:T(8,128)(2,1)S(1)} %all_to_all.19), kind=kOutput, calls=%fused_computation.14 | convolution fusion | flops 2147483648 | bytes 8388608 | tf_op jit(solution)/shard_map/dot_general | solution.py:10
  49.3 1.8 collective-permute-done
  51.1 2.3 %fusion.28 = f32[512,1024]{1,0:T(8,128)S(1)} fusion(bf16[512,2048]{1,0:T(8,128)(2,1)S(1)} %collective-permute-done, bf16[2048,1024]{1,0:T(8,128)(2,1)S(1)} %copy-done.3), kind=kOutput, calls=%fused_computation.44 | convolution fusion | flops 2147483648 | bytes 8388608 | tf_op jit(solution)/shard_map/dot_general | solution.py:10
  53.5 0.6 pad_maximum_fusion
  54.1 2.3 %copy.17 = f32[4,2,128,1024]{3,2,1,0:T(8,128)} copy(f32[4,2,128,1024]{3,2,0,1:T(8,128)S(1)} %pad_maximum_fusion) | data formatting | bytes 8388608 | tf_op jit(solution)/shard_map/concatenate | solution.py:36
  56.4 0.0 reduce-scatter.3.cloned.1.call-update
  56.4 0.0 all-gather.3.cloned.1.call-start
  56.5 0.6 copy-done.1
  57.1 0.0 copy-done.2
  57.2 51.9 %reduce-scatter.3.cloned.1.call-done = f32[256,1024]{1,0:T(8,128)} async-done(((f32[1024,1024]{1,0:T(8,128)}), f32[256,1024]{1,0:T(8,128)}) %reduce-scatter.3.cloned.1.call-update) | async-done | bytes 1048592 | tf_op jit(solution)/shard_map/reduce_scatter | solution.py:34
  109.0 1.4 reduce_max.18
  110.4 1.6 exponential_reduce_fusion
  112.0 14.0 %all-gather = f32[24,2,128]{2,1,0:T(2,128)S(1)} all-gather(f32[3,2,128]{2,1,0:T(2,128)S(1)} %broadcast_select_fusion), channel_id=2, replica_groups=mesh['dp'=4,'z'=4,'core'=2] {'z','core'}, dimensions={0}, use_global_device_ids=true | all-gather | bytes 27648 | tf_op jit(solution)/shard_map/all_gather | solution.py:46
  126.2 0.6 select_divide_fusion
  126.8 2.4 %multiply_convert_fusion = bf16[1,2,128,1024]{3,2,1,0:T(8,128)(2,1)} fusion(f32[1,2,128,1024]{3,2,1,0:T(8,128)} %bitcast.63, s32[1024]{0:T(1024)S(1)} %iota_add_fusion, s32[2,128]{1,0:T(2,128)S(1)} %get-tuple-element.11, f32[2,128]{1,0:T(2,128)S(1)} %get-tuple-element.7, f32[2,128]{1,0:T(2,128)S(1)} %bitcast.78, f32[2,128]{1,0:T(2,128)S(1)} %pad_maximum_fusion.2), kind=kLoop, calls=%fused_computation.15 | loop fusion | flops 1835008 | bytes 1581056 | tf_op jit(solution)/shard_map/convert_element_type | solution.py:55
  129.2 0.0 all-gather.3.cloned.1.call-update
  129.2 0.2 reduce-scatter.5.cloned.1.call-start
  129.4 34.9 %all-gather.3.cloned.1.call-done = bf16[4,2,128,1024]{3,2,1,0:T(8,128)(2,1)} async-done(((bf16[1,2,128,1024]{3,2,1,0:T(8,128)(2,1)}), bf16[4,2,128,1024]{3,2,1,0:T(8,128)(2,1)}) %all-gather.3.cloned.1.call-update) | async-done | bytes 2097168 | tf_op jit(solution)/shard_map/all_gather | solution.py:56
  164.4 1.9 fusion.27
  166.3 0.9 copy-done.4
  167.2 2.4 %convolution_convert_fusion = bf16[512,2048]{1,0:T(8,128)(2,1)S(1)} fusion(bf16[512,1024]{1,0:T(8,128)(2,1)S(1)} %bitcast.69, bf16[2048,1024]{1,0:T(8,128)(2,1)S(1)} %copy-done.4), kind=kOutput, calls=%fused_computation.9 | convolution fusion | flops 2148532224 | bytes 7340032 | tf_op jit(solution)/shard_map/dot_general | solution.py:14
  169.6 0.1 collective-permute-start.1
  169.7 4.1 %collective-permute-done.1 = bf16[512,2048]{1,0:T(8,128)(2,1)S(1)} collective-permute-done((bf16[512,2048]{1,0:T(8,128)(2,1)S(1)}, bf16[512,2048]{1,0:T(8,128)(2,1)S(1)}, u32[]{:S(2)}, u32[]{:S(2)}) %collective-permute-start.1) | collective-permute-done | bytes 2097184 | tf_op jit(solution)/shard_map/ppermute | solution.py:59
  173.8 3.7 %add_convert_fusion = bf16[512,2048]{1,0:T(8,128)(2,1)} fusion(bf16[512,2048]{1,0:T(8,128)(2,1)S(1)} %collective-permute-done.1, bf16[512,1024]{1,0:T(8,128)(2,1)S(1)} %bitcast.71, bf16[2048,1024]{1,0:T(8,128)(2,1)S(1)} %copy-done.4), kind=kOutput, calls=%fused_computation.7 | convolution fusion | flops 2150629376 | bytes 9437184 | tf_op jit(solution)/shard_map/dot_general | solution.py:14
  177.5 0.0 reduce-scatter.5.cloned.1.call-update
  177.5 8.4 %fusion.6 = bf16[2048,1024]{1,0:T(8,128)(2,1)} fusion(bf16[512,2048]{1,0:T(8,128)(2,1)} %copy-done.5, bf16[512,2048]{1,0:T(8,128)(2,1)S(1)} %bitcast.66, bf16[512,1024]{1,0:T(8,128)(2,1)S(1)} %bitcast.70, bf16[512,1024]{1,0:T(8,128)(2,1)} %bitcast.72), kind=kOutput, calls=%fused_computation.8 | convolution fusion | flops 4309647360 | bytes 10485760 | tf_op jit(solution)/shard_map/dot_general | solution.py:62
  186.0 35.3 %reduce-scatter.5.cloned.1.call-done = bf16[128,2048]{1,0:T(8,128)(2,1)} async-done(((bf16[512,2048]{1,0:T(8,128)(2,1)}), bf16[128,2048]{1,0:T(8,128)(2,1)}) %reduce-scatter.5.cloned.1.call-update) | async-done | bytes 524304 | tf_op jit(solution)/shard_map/reduce_scatter | solution.py:61
  (23 shorter events, 0.2 us)
Async XLA Ops:
  7.2 101.9 %reduce-scatter.3.cloned.1.call-start = ((), (), s32[]{:S(2)}) async-start(), calls=%async_computation.3 | async-start | bytes 5242880 | tf_op jit(solution)/shard_map/reduce_scatter | solution.py:34
  16.1 30.8 %copy-start.3 = (bf16[2048,1024]{1,0:T(8,128)(2,1)S(1)}, bf16[2048,1024]{1,0:T(8,128)(2,1)}, u32[]{:S(2)}) copy-start(bf16[2048,1024]{1,0:T(8,128)(2,1)} %param.5) | copy-start | bytes 12582916
  47.0 4.2 %collective-permute-start = (bf16[512,2048]{1,0:T(8,128)(2,1)S(1)}, bf16[512,2048]{1,0:T(8,128)(2,1)S(1)}, u32[]{:S(2)}, u32[]{:S(2)}) collective-permute-start(bf16[512,2048]{1,0:T(8,128)(2,1)S(1)} %bitcast.65), channel_id=1, source_target_pairs={{0,1},{1,0},{2,3},{3,2},{4,5},{5,4},{6,7},{7,6},{8,9},{9,8},{10,11... | collective-permute-start | bytes 6291464 | tf_op jit(solution)/shard_map/ppermute | solution.py:30
  51.1 2.4 %copy-start.5 = (bf16[512,2048]{1,0:T(8,128)(2,1)}, bf16[512,2048]{1,0:T(8,128)(2,1)S(1)}, u32[]{:S(2)}) copy-start(bf16[512,2048]{1,0:T(8,128)(2,1)S(1)} %collective-permute-done) | copy-start | bytes 6291460
  56.4 0.7 copy-start.1
  56.4 0.7 copy-start.2
  56.4 107.9 %all-gather.3.cloned.1.call-start = ((), (), s32[]{:S(2)}) async-start(), calls=%async_computation.4 | async-start | bytes 2621440 | tf_op jit(solution)/shard_map/all_gather | solution.py:56
  129.2 92.1 %reduce-scatter.5.cloned.1.call-start = ((), (), s32[]{:S(2)}) async-start(), calls=%async_computation.5 | async-start | bytes 2621440 | tf_op jit(solution)/shard_map/reduce_scatter | solution.py:61
  164.4 2.8 %copy-start.4 = (bf16[2048,1024]{1,0:T(8,128)(2,1)S(1)}, bf16[2048,1024]{1,0:T(8,128)(2,1)}, u32[]{:S(2)}) copy-start(bf16[2048,1024]{1,0:T(8,128)(2,1)} %param.5) | copy-start | bytes 12582916
  166.2 7.6 %copy-start = (bf16[4,1,128,1024]{3,2,1,0:T(8,128)(2,1)}, bf16[4,1,128,1024]{3,2,1,0:T(8,128)(2,1)S(1)}, u32[]{:S(2)}) copy-start(bf16[4,1,128,1024]{3,2,1,0:T(8,128)(2,1)S(1)} %get-tuple-element.6) | copy-start | bytes 3145732
  169.6 4.2 %collective-permute-start.1 = (bf16[512,2048]{1,0:T(8,128)(2,1)S(1)}, bf16[512,2048]{1,0:T(8,128)(2,1)S(1)}, u32[]{:S(2)}, u32[]{:S(2)}) collective-permute-start(bf16[512,2048]{1,0:T(8,128)(2,1)S(1)} %convolution_convert_fusion), channel_id=1, source_target_pairs={{0,1},{1,0},{2,3},{3,2},{4,5},{5,4},{6,7},{7,6},{8,9},{9,8},{10,11... | collective-permute-start | bytes 6291464 | tf_op jit(solution)/shard_map/ppermute | solution.py:59
Sparse Core Ops, SparseCore 0:
  56.6 52.4 reduce-scatter.2
  129.3 35.0 all-gather.2
  177.6 43.6 reduce-scatter.4

commit v2 on v1

v2 whole, which is shorter than its diff:
```python
import jax
import jax.numpy as jnp
from jax import lax
from jax.sharding import Mesh, PartitionSpec as P

CORES = 2


def forward_dot(rows, weight):
    return jnp.dot(rows, weight, preferred_element_type=jnp.float32)


def hidden_dot(grads, weight):
    return lax.dot_general(grads, weight, (((1,), (1,)), ((), ())), preferred_element_type=jnp.float32)


def shards(hidden, weight, targets, cotangent):
    dp, deep = lax.axis_size("dp"), lax.axis_size("z")
    own, vocab_width = hidden.shape[0], weight.shape[1]
    block = own * dp // (deep * CORES)
    core = lax.axis_index("core")
    swap = [(0, 1), (1, 0)]

    def halves(x):
        parts = x.reshape((own // (CORES * block), CORES, block) + x.shape[1:])
        pick = lambda c: lax.dynamic_index_in_dim(parts, c, 1, keepdims=False).reshape((own // CORES,) + x.shape[1:])
        return pick(core), pick(1 - core)

    me = lax.axis_index("dp")
    width = weight.shape[0]

    def swing(x, k):
        return lax.ppermute(x, "dp", [(i, i ^ k) for i in range(dp)])

    share = halves(hidden)[0]

    def column_block(k):
        return lax.dynamic_slice_in_dim(share, (me ^ k) * width, width, axis=1)

    mine = [column_block(0)] + [swing(column_block(k), k) for k in range(1, dp)]
    other = [lax.ppermute(x, "core", swap) for x in mine]
    part_rows = mine[0].shape[0]

    def partials(blocks, bit):
        sets = [[k for k in range(dp) if bool(k & bit) == flag] for flag in (True, False)]
        made = [None] * dp
        for keys in sets:
            out = forward_dot(jnp.concatenate([blocks[k] for k in keys]), weight)
            for n, k in enumerate(keys):
                made[k] = out[n * part_rows:(n + 1) * part_rows]
        return made

    bits = [1 << n for n in range(dp.bit_length() - 1)]

    def reduce_blocks(blocks, order):
        held = dict(enumerate(partials(blocks, order[0])))
        for bit in order:
            sent = {k: swing(held[k], bit) for k in held if k & bit}
            held = {k: held[k] + sent[k | bit] for k in held if not k & bit}
        return held[0]

    logits = jnp.stack([reduce_blocks(mine, bits), reduce_blocks(other, bits[::-1])])
    goal = jnp.stack(halves(targets))
    cot = jnp.stack(halves(cotangent))
    first = (lax.axis_index("z") * CORES + core) * vocab_width
    onehot = (goal[:, :, None] == first + lax.iota(jnp.int32, vocab_width)).astype(jnp.float32)
    local_max = jnp.max(logits, axis=2)
    shifted = jnp.exp(logits - local_max[:, :, None])
    local = jnp.stack([local_max, jnp.sum(shifted, axis=2), jnp.sum(logits * onehot, axis=2)])
    depth = lax.axis_index("z")
    partner = lax.ppermute(local, "core", swap)[:, ::-1]
    pair = jnp.where(core == 0, jnp.stack([local, partner]), jnp.stack([partner, local]))
    pair_max = jnp.max(pair[:, 0], axis=0)
    pair_sum = jnp.sum(pair[:, 1] * jnp.exp(pair[:, 0] - pair_max), axis=0)
    merged = jnp.stack([pair_max, pair_sum, jnp.sum(pair[:, 2], axis=0)])
    ring = jnp.stack([merged] + [lax.ppermute(merged, "z", [((i + n) % deep, i) for i in range(deep)]) for n in range(1, deep)])
    every = jnp.stack([lax.dynamic_index_in_dim(ring, (i - depth) % deep, 0, keepdims=False) for i in range(deep)])
    maxima = every[:, 0]
    row_max = jnp.max(maxima, axis=0)
    sum_exp = jnp.sum(every[:, 1] * jnp.exp(maxima - row_max), axis=0)
    loss = row_max + jnp.log(sum_exp) - jnp.sum(every[:, 2], axis=0)
    loss = jnp.where(core == 0, loss, loss[::-1])
    loss = loss.reshape(CORES, own // (CORES * block), block).swapaxes(0, 1).reshape(own)
    scale = jnp.exp(local_max - row_max) / sum_exp
    grads = (cot[:, :, None] * (shifted * scale[:, :, None] - onehot)).astype(jnp.bfloat16)

    def spread_out(block, order):
        held = {0: block}
        for bit in order:
            held.update({k | bit: swing(x, bit) for k, x in list(held.items())})
        return [held[k] for k in range(dp)]

    other_grads = spread_out(grads[1], bits[::-1])
    mine_grads = spread_out(grads[0], bits)
    near_mine, near_other = jnp.stack(mine_grads), jnp.stack(other_grads)
    per = deep // dp

    def chunk(near, r):
        d = (depth + r) % deep
        return lax.dynamic_slice(near, (me ^ (d // per), (d % per) * block, 0), (1, block, vocab_width))[0]

    def share_of(r):
        away = lax.ppermute(hidden_dot(chunk(near_other, r), weight), "core", swap)
        return hidden_dot(chunk(near_mine, r), weight) + away

    shares = {}
    for n in range(1, deep // 2 + 1):
        for r in (deep - n, n):
            if r not in shares:
                shares[r] = share_of(r)
    shares[0] = share_of(0)
    cut = width // 2
    ups, downs = [(i, (i + 1) % deep) for i in range(deep)], [(i, (i - 1) % deep) for i in range(deep)]
    up, down = shares[deep - 1][:, :cut], shares[1][:, cut:]
    for n in range(1, deep):
        up = lax.ppermute(up.astype(jnp.bfloat16), "z", ups).astype(jnp.float32) + shares[(deep - 1 - n) % deep][:, :cut]
        down = lax.ppermute(down.astype(jnp.bfloat16), "z", downs).astype(jnp.float32) + shares[(1 + n) % deep][:, cut:]
    grad_hidden = jnp.concatenate([up, down], axis=1).astype(jnp.bfloat16)
    weigh = lambda h, g: lax.dot_general(h, g, (((0,), (0,)), ((), ())), preferred_element_type=jnp.float32)
    rows = jnp.concatenate(mine + other)
    columns = jnp.concatenate(mine_grads + other_grads)
    grad_weight = weigh(rows, columns).astype(jnp.bfloat16)
    return (loss, grad_hidden, grad_weight)


def solution(mesh):
    dp, vocab = mesh.shape["dp"], mesh.shape["vocab"]
    fine = Mesh(mesh.devices.reshape(dp, vocab // CORES, CORES), ("dp", "z", "core"))
    cols = ("z", "core")
    in_specs = (P("dp", None), P("dp", cols), P("dp"), P("dp"))
    out_specs = (P("dp"), P(cols, "dp"), P("dp", cols))
    return jax.shard_map(shards, mesh=fine, in_specs=in_specs, out_specs=out_specs, check_vma=False)
```

time: 228 us -> 170 us (0.75)
  blocking collectives: 44.9 us -> 0 us
  waiting for transfers between devices: 128 us -> 91.1 us
  starting transfers between devices: 0.38 us -> 32.9 us
  between operations: 13.9 us -> 1.16 us
  matrix products: 19.2 us -> 27.8 us
  other arithmetic: 6.62 us -> 3.5 us
    reduce_scatter x2 -> x0, waiting for transfers between devices: 87.2 us -> none  [the longest x1 51.9 us: scatter(): return lax.psum_scatter(part, 'dp', scatter_dimension=0, tiled=True)]
    ppermute x2 -> x33, waiting for transfers between devices: 5.93 us -> 91.1 us  [the longest x15 63.3 us: swing(): return lax.ppermute(x, 'dp', [(i, i ^ k) for i in range(dp)])]
    all_gather x1 -> x0, waiting for transfers between devices: 34.9 us -> none  [shards(): gathered = lax.all_gather(grads, 'dp', axis=0, tiled=False)]
    ppermute x2 -> x33, starting transfers between devices: 0.07 us -> 32.9 us  [the longest x15 16.9 us: swing(): return lax.ppermute(x, 'dp', [(i, i ^ k) for i in range(dp)])]
    all_to_all x1 -> x0, blocking collectives: 30.8 us -> none  [shards(): lax.all_to_all(halves(hidden)[0], 'dp', split_axis=1, concat_axis=0, tile...]
    all_gather x1 -> x0, blocking collectives: 14 us -> none  [shards(): every = lax.all_gather(order, ('z', 'core'), axis=0)]
    dot_general x2 -> x8, matrix products: 6.06 us -> 14.3 us  [hidden_dot(): lax.dot_general(grads, weight, (((1,), (1,)), ((), ())), preferred_elemen...]
    unnamed x12 -> x26, local copies, waits for them, and re-layouts: 1.55 us -> 9.37 us
  transfers between devices with their start and end apart: 5 -> 33, of which waited for: 5 -> 21; matrix products, arithmetic and copies ran while one was open for 5% -> 23% of each run, Pallas kernels for 0% -> 0%
where the time goes in v2:
time: 170 us
  waiting for transfers between devices  91.1 us (54%)
  starting transfers between devices  32.9 us (19%)
  matrix products  27.8 us (16%)
  local copies, waits for them, and re-layouts  13.7 us (8%)
  other arithmetic  3.5 us (2%)
    ppermute x15, waiting for transfers between devices, swing(): return lax.ppermute(x, 'dp', [(i, i ^ k) for i in range(dp)])  63.3 us
    ppermute x15, starting transfers between devices, swing(): return lax.ppermute(x, 'dp', [(i, i ^ k) for i in range(dp)])  16.9 us
    dot_general x8, matrix products, hidden_dot(): lax.dot_general(grads, weight, (((1,), (1,)), ((), ())), preferred_elemen...  14.3 us
    ppermute x3, waiting for transfers between devices, shards(): lax.ppermute(down.astype(jnp.bfloat16), 'z', downs).astype(jnp.float32)  11.7 us
    unnamed x26, local copies, waits for them, and re-layouts  9.37 us
    ppermute x3, starting transfers between devices, shards(): lax.ppermute(down.astype(jnp.bfloat16), 'z', downs).astype(jnp.float32)  9.36 us
    ppermute x3, waiting for transfers between devices, shards(): lax.ppermute(up.astype(jnp.bfloat16), 'z', ups).astype(jnp.float32)  9.03 us
    dot_general x4, matrix products, forward_dot(): return jnp.dot(rows, weight, preferred_element_type=jnp.float32)  7.27 us
  transfers between devices with their start and end apart: 33, of which 21 were waited for; matrix products, arithmetic and copies ran while one was open for 23% of the time, Pallas kernels for 0%

profile of v2, /device:TPU:0, one launch (start us, length us, event | category | flops | bytes accessed | tf_op | source)
XLA Modules:
  0.0 170.1 jit_solution(4402115556280921417)
XLA Ops:
  0.7 3.0 %dynamic-slice_bitcast_fusion.1 = (bf16[128,2048]{1,0:T(8,128)(2,1)}, bf16[128,2048]{1,0:T(8,128)(2,1)}, bf16[128,2048]{1,0:T(8,128)(2,1)S(1)}) fusion(bf16[1,2,128,8192]{3,2,1,0:T(8,128)(2,1)} %bitcast.120, s32[]{:T(128)S(6)} %select_n.158, s32[]{:T(128)S(6)} %select_n.164, s32[]{:T(128)S(6)} %select_n.166, s32[]{:T(128)S(6)} %select_n.162), kind=kLoop, calls=%fused_computation.56 | loop fusion | bytes 3145744 | tf_op jit(solution)/shard_map/dynamic_slice | solution.py:38
  3.7 3.0 %collective-permute-start.1 = (bf16[128,2048]{1,0:T(8,128)(2,1)}, bf16[128,2048]{1,0:T(8,128)(2,1)S(1)}, u32[]{:S(2)}, u32[]{:S(2)}) collective-permute-start(bf16[128,2048]{1,0:T(8,128)(2,1)} %get-tuple-element.7), channel_id=1, source_target_pairs={{0,8},{8,0},{16,24},{24,16},{1,9},{9,1},{17,25},{25,17},{2,10},{10... | collective-permute-start | bytes 1572872 | tf_op jit(solution)/shard_map/ppermute | solution.py:33
  8.2 2.1 %constant_dynamic-update-slice_fusion.7 = (bf16[1024,2048]{1,0:T(8,128)(2,1)}, bf16[128,2048]{1,0:T(8,128)(2,1)S(1)}) fusion(bf16[1,2,128,8192]{3,2,1,0:T(8,128)(2,1)} %bitcast.121, s32[]{:T(128)S(6)} %select_n.158, s32[]{:T(128)S(6)} %select_n.160), kind=kLoop, calls=%fused_computation.87 | loop fusion | bytes 1572872
  10.4 9.2 %collective-permute-done.1 = bf16[128,2048]{1,0:T(8,128)(2,1)S(1)} collective-permute-done((bf16[128,2048]{1,0:T(8,128)(2,1)}, bf16[128,2048]{1,0:T(8,128)(2,1)S(1)}, u32[]{:S(2)}, u32[]{:S(2)}) %collective-permute-start.1) | collective-permute-done | bytes 524320 | tf_op jit(solution)/shard_map/ppermute | solution.py:33
  19.7 11.7 %collective-permute-done.2 = bf16[128,2048]{1,0:T(8,128)(2,1)S(1)} collective-permute-done((bf16[128,2048]{1,0:T(8,128)(2,1)}, bf16[128,2048]{1,0:T(8,128)(2,1)S(1)}, u32[]{:S(2)}, u32[]{:S(2)}) %collective-permute-start.2) | collective-permute-done | bytes 524320 | tf_op jit(solution)/shard_map/ppermute | solution.py:33
  31.3 3.4 %fusion.8 = f32[256,1024]{1,0:T(8,128)S(1)} fusion(bf16[2048,1024]{1,0:T(8,128)(2,1)} %param.5, bf16[128,2048]{1,0:T(8,128)(2,1)S(1)} %collective-permute-done.2, bf16[128,2048]{1,0:T(8,128)(2,1)S(1)} %collective-permute-done.1), kind=kOutput, calls=%fused_computation.15 | convolution fusion | flops 1075838976 | bytes 6291456 | tf_op jit(solution)/shard_map/dot_general | solution.py:10
  34.9 1.6 collective-permute-start.3
  43.9 1.8 %collective-permute-start.11 = (f32[128,1024]{1,0:T(8,128)S(1)}, f32[128,1024]{1,0:T(8,128)S(1)}, u32[]{:S(2)}, u32[]{:S(2)}) collective-permute-start(f32[128,1024]{1,0:T(8,128)S(1)} %get-tuple-element.17), channel_id=1, source_target_pairs={{0,16},{8,24},{16,0},{24,8},{1,17},{9,25},{17,1},{25,9},{2,18},{10... | collective-permute-start | bytes 1572872 | tf_op jit(solution)/shard_map/ppermute | solution.py:33
  45.7 13.3 %collective-permute-done.4 = f32[128,1024]{1,0:T(8,128)S(1)} collective-permute-done((f32[128,1024]{1,0:T(8,128)S(1)}, f32[128,1024]{1,0:T(8,128)S(1)}, u32[]{:S(2)}, u32[]{:S(2)}) %collective-permute-start.4) | collective-permute-done | bytes 524320 | tf_op jit(solution)/shard_map/ppermute | solution.py:33
  60.9 8.7 %collective-permute-done.11 = f32[128,1024]{1,0:T(8,128)S(1)} collective-permute-done((f32[128,1024]{1,0:T(8,128)S(1)}, f32[128,1024]{1,0:T(8,128)S(1)}, u32[]{:S(2)}, u32[]{:S(2)}) %collective-permute-start.11) | collective-permute-done | bytes 524320 | tf_op jit(solution)/shard_map/ppermute | solution.py:33
  69.7 1.6 collective-permute-start.12
  72.9 7.5 %collective-permute-done.5 = f32[128,1024]{1,0:T(8,128)S(1)} collective-permute-done((f32[128,1024]{1,0:T(8,128)S(1)}, f32[128,1024]{1,0:T(8,128)S(1)}, u32[]{:S(2)}, u32[]{:S(2)}) %collective-permute-start.5) | collective-permute-done | bytes 524320 | tf_op jit(solution)/shard_map/ppermute | solution.py:33
  80.5 2.3 %collective-permute-done.12 = f32[128,1024]{1,0:T(8,128)S(1)} collective-permute-done((f32[128,1024]{1,0:T(8,128)S(1)}, f32[128,1024]{1,0:T(8,128)S(1)}, u32[]{:S(2)}, u32[]{:S(2)}) %collective-permute-start.12) | collective-permute-done | bytes 524320 | tf_op jit(solution)/shard_map/ppermute | solution.py:33
  84.8 2.6 %collective-permute-start.15 = (f32[3,2,128]{2,1,0:T(2,128)S(1)}, f32[3,2,128]{2,1,0:T(2,128)S(1)}, u32[]{:S(2)}, u32[]{:S(2)}) collective-permute-start(f32[3,2,128]{2,1,0:T(2,128)S(1)} %pad_maximum_fusion.7), channel_id=1, source_target_pairs={{4,0},{6,2},{0,4},{2,6},{5,1},{7,3},{1,5},{3,7},{12,8},{14,10},{8,... | collective-permute-start | bytes 9224 | tf_op jit(solution)/shard_map/ppermute | solution.py:76
  89.5 1.6 collective-permute-done.14
  91.0 3.2 %collective-permute-done.16 = f32[3,2,128]{2,1,0:T(2,128)S(1)} collective-permute-done((f32[3,2,128]{2,1,0:T(2,128)S(1)}, f32[3,2,128]{2,1,0:T(2,128)S(1)}, u32[]{:S(2)}, u32[]{:S(2)}) %collective-permute-start.16) | collective-permute-done | bytes 3104 | tf_op jit(solution)/shard_map/ppermute | solution.py:76
  96.2 1.5 collective-permute-start.18
  100.5 3.5 %collective-permute-done.21 = bf16[128,1024]{1,0:T(8,128)(2,1)S(1)} collective-permute-done((bf16[128,1024]{1,0:T(8,128)(2,1)S(1)}, bf16[128,1024]{1,0:T(8,128)(2,1)S(1)}, u32[]{:S(2)}, u32[]{:S(2)}) %collective-permute-start.21) | collective-permute-done | bytes 262176 | tf_op jit(solution)/shard_map/ppermute | solution.py:33
  108.2 1.5 collective-permute-done.18
  110.4 1.9 %collective-permute-done.20 = bf16[128,1024]{1,0:T(8,128)(2,1)S(1)} collective-permute-done((bf16[128,1024]{1,0:T(8,128)(2,1)S(1)}, bf16[128,1024]{1,0:T(8,128)(2,1)S(1)}, u32[]{:S(2)}, u32[]{:S(2)}) %collective-permute-start.20) | collective-permute-done | bytes 262176 | tf_op jit(solution)/shard_map/ppermute | solution.py:33
  112.3 2.8 %collective-permute-done.22 = bf16[128,1024]{1,0:T(8,128)(2,1)S(1)} collective-permute-done((bf16[128,1024]{1,0:T(8,128)(2,1)S(1)}, bf16[128,1024]{1,0:T(8,128)(2,1)S(1)}, u32[]{:S(2)}, u32[]{:S(2)}) %collective-permute-start.22) | collective-permute-done | bytes 262176 | tf_op jit(solution)/shard_map/ppermute | solution.py:33
  115.2 3.7 %fusion.35 = f32[128,2048]{1,0:T(8,128)S(1)} fusion(bf16[2048,1024]{1,0:T(8,128)(2,1)} %param.5, bf16[4,128,1024]{2,1,0:T(8,128)(2,1)S(1)} %pad_maximum_fusion.2, s32[]{:T(128)S(6)} %select_n.183), kind=kOutput, calls=%fused_computation.63 | convolution fusion | flops 536870912 | bytes 5505028 | tf_op jit(solution)/shard_map/dot_general | solution.py:14
  129.3 2.7 %collective-permute-start.30 = (bf16[128,1024]{1,0:T(8,128)(2,1)S(1)}, bf16[128,1024]{1,0:T(8,128)(2,1)S(1)}, u32[]{:S(2)}, u32[]{:S(2)}) collective-permute-start(bf16[128,1024]{1,0:T(8,128)(2,1)S(1)} %slice.175), channel_id=1, source_target_pairs={{0,6},{2,0},{4,2},{6,4},{1,7},{3,1},{5,3},{7,5},{8,14},{10,8},{12,... | collective-permute-start | bytes 786440 | tf_op jit(solution)/shard_map/ppermute | solution.py:117
  132.0 1.5 convolution_add_fusion.2
  133.6 4.1 %collective-permute-done.24 = bf16[128,1024]{1,0:T(8,128)(2,1)S(1)} collective-permute-done((bf16[128,1024]{1,0:T(8,128)(2,1)S(1)}, bf16[128,1024]{1,0:T(8,128)(2,1)S(1)}, u32[]{:S(2)}, u32[]{:S(2)}) %collective-permute-start.24) | collective-permute-done | bytes 262176 | tf_op jit(solution)/shard_map/ppermute | solution.py:116
  137.7 4.7 %collective-permute-done.30 = bf16[128,1024]{1,0:T(8,128)(2,1)S(1)} collective-permute-done((bf16[128,1024]{1,0:T(8,128)(2,1)S(1)}, bf16[128,1024]{1,0:T(8,128)(2,1)S(1)}, u32[]{:S(2)}, u32[]{:S(2)}) %collective-permute-start.30) | collective-permute-done | bytes 262176 | tf_op jit(solution)/shard_map/ppermute | solution.py:117
  142.6 3.8 %collective-permute-start.31 = (bf16[128,1024]{1,0:T(8,128)(2,1)S(1)}, bf16[128,1024]{1,0:T(8,128)(2,1)S(1)}, u32[]{:S(2)}, u32[]{:S(2)}) collective-permute-start(bf16[128,1024]{1,0:T(8,128)(2,1)S(1)} %get-tuple-element.13), channel_id=1, source_target_pairs={{0,6},{2,0},{4,2},{6,4},{1,7},{3,1},{5,3},{7,5},{8,14},{10,8},{12,... | collective-permute-start | bytes 786440 | tf_op jit(solution)/shard_map/ppermute | solution.py:117
  146.4 6.2 %convolution_convert_fusion = bf16[2048,1024]{1,0:T(8,128)(2,1)} fusion(bf16[1024,2048]{1,0:T(8,128)(2,1)S(1)} %copy-done.2, bf16[1024,1024]{1,0:T(8,128)(2,1)S(1)} %constant_dynamic-update-slice_fusion.8), kind=kOutput, calls=%fused_computation | convolution fusion | flops 4297064448 | bytes 10485760 | tf_op jit(solution)/shard_map/dot_general | solution.py:119
  153.8 2.8 %collective-permute-done.31 = bf16[128,1024]{1,0:T(8,128)(2,1)S(1)} collective-permute-done((bf16[128,1024]{1,0:T(8,128)(2,1)S(1)}, bf16[128,1024]{1,0:T(8,128)(2,1)S(1)}, u32[]{:S(2)}, u32[]{:S(2)}) %collective-permute-start.31) | collective-permute-done | bytes 262176 | tf_op jit(solution)/shard_map/ppermute | solution.py:117
  156.6 2.8 %collective-permute-start.32 = (bf16[128,1024]{1,0:T(8,128)(2,1)S(1)}, bf16[128,1024]{1,0:T(8,128)(2,1)S(1)}, u32[]{:S(2)}, u32[]{:S(2)}) collective-permute-start(bf16[128,1024]{1,0:T(8,128)(2,1)S(1)} %fusion.22), channel_id=1, source_target_pairs={{0,6},{2,0},{4,2},{6,4},{1,7},{3,1},{5,3},{7,5},{8,14},{10,8},{12,... | collective-permute-start | bytes 786440 | tf_op jit(solution)/shard_map/ppermute | solution.py:117
  160.9 4.0 %collective-permute-done.28 = bf16[128,1024]{1,0:T(8,128)(2,1)S(1)} collective-permute-done((bf16[128,1024]{1,0:T(8,128)(2,1)S(1)}, bf16[128,1024]{1,0:T(8,128)(2,1)S(1)}, u32[]{:S(2)}, u32[]{:S(2)}) %collective-permute-start.28) | collective-permute-done | bytes 262176 | tf_op jit(solution)/shard_map/ppermute | solution.py:116
  164.9 4.2 %collective-permute-done.32 = bf16[128,1024]{1,0:T(8,128)(2,1)S(1)} collective-permute-done((bf16[128,1024]{1,0:T(8,128)(2,1)S(1)}, bf16[128,1024]{1,0:T(8,128)(2,1)S(1)}, u32[]{:S(2)}, u32[]{:S(2)}) %collective-permute-start.32) | collective-permute-done | bytes 262176 | tf_op jit(solution)/shard_map/ppermute | solution.py:117
  (118 shorter events, 40.6 us)
Async XLA Ops:
  3.7 15.9 %collective-permute-start.1 = (bf16[128,2048]{1,0:T(8,128)(2,1)}, bf16[128,2048]{1,0:T(8,128)(2,1)S(1)}, u32[]{:S(2)}, u32[]{:S(2)}) collective-permute-start(bf16[128,2048]{1,0:T(8,128)(2,1)} %get-tuple-element.7), channel_id=1, source_target_pairs={{0,8},{8,0},{16,24},{24,16},{1,9},{9,1},{17,25},{25,17},{2,10},{10... | collective-permute-start | bytes 1572872 | tf_op jit(solution)/shard_map/ppermute | solution.py:33
  6.7 24.7 %collective-permute-start.2 = (bf16[128,2048]{1,0:T(8,128)(2,1)}, bf16[128,2048]{1,0:T(8,128)(2,1)S(1)}, u32[]{:S(2)}, u32[]{:S(2)}) collective-permute-start(bf16[128,2048]{1,0:T(8,128)(2,1)} %get-tuple-element.8), channel_id=1, source_target_pairs={{0,24},{8,16},{16,8},{24,0},{1,25},{9,17},{17,9},{25,1},{2,26},{10... | collective-permute-start | bytes 1572872 | tf_op jit(solution)/shard_map/ppermute | solution.py:33
  8.2 29.7 %collective-permute-start = (bf16[128,2048]{1,0:T(8,128)(2,1)S(1)}, bf16[128,2048]{1,0:T(8,128)(2,1)S(1)}, u32[]{:S(2)}, u32[]{:S(2)}) collective-permute-start(bf16[128,2048]{1,0:T(8,128)(2,1)S(1)} %get-tuple-element.9), channel_id=1, source_target_pairs={{0,16},{8,24},{16,0},{24,8},{1,17},{9,25},{17,1},{25,9},{2,18},{10... | collective-permute-start | bytes 1572872 | tf_op jit(solution)/shard_map/ppermute | solution.py:33
  10.3 29.7 %collective-permute-start.6 = (bf16[128,2048]{1,0:T(8,128)(2,1)S(1)}, bf16[128,2048]{1,0:T(8,128)(2,1)S(1)}, u32[]{:S(2)}, u32[]{:S(2)}) collective-permute-start(bf16[128,2048]{1,0:T(8,128)(2,1)S(1)} %get-tuple-element.6), channel_id=1, source_target_pairs={{0,1},{1,0},{2,3},{3,2},{4,5},{5,4},{6,7},{7,6},{8,9},{9,8},{10,11... | collective-permute-start | bytes 1572872 | tf_op jit(solution)/shard_map/ppermute | solution.py:41
  34.9 38.0 %collective-permute-start.3 = (f32[128,1024]{1,0:T(8,128)S(1)}, f32[128,1024]{1,0:T(8,128)S(1)}, u32[]{:S(2)}, u32[]{:S(2)}) collective-permute-start(f32[128,1024]{1,0:T(8,128)S(1)} %get-tuple-element.14), channel_id=1, source_target_pairs={{0,8},{8,0},{16,24},{24,16},{1,9},{9,1},{17,25},{25,17},{2,10},{10... | collective-permute-start | bytes 1572872 | tf_op jit(solution)/shard_map/ppermute | solution.py:33
  36.5 22.5 %collective-permute-start.4 = (f32[128,1024]{1,0:T(8,128)S(1)}, f32[128,1024]{1,0:T(8,128)S(1)}, u32[]{:S(2)}, u32[]{:S(2)}) collective-permute-start(f32[128,1024]{1,0:T(8,128)S(1)} %get-tuple-element.15), channel_id=1, source_target_pairs={{0,8},{8,0},{16,24},{24,16},{1,9},{9,1},{17,25},{25,17},{2,10},{10... | collective-permute-start | bytes 1572872 | tf_op jit(solution)/shard_map/ppermute | solution.py:33
  37.0 22.6 %collective-permute-start.7 = (bf16[128,2048]{1,0:T(8,128)(2,1)S(1)}, bf16[128,2048]{1,0:T(8,128)(2,1)S(1)}, u32[]{:S(2)}, u32[]{:S(2)}) collective-permute-start(bf16[128,2048]{1,0:T(8,128)(2,1)S(1)} %collective-permute-done.1), channel_id=1, source_target_pairs={{0,1},{1,0},{2,3},{3,2},{4,5},{5,4},{6,7},{7,6},{8,9},{9,8},{10,11... | collective-permute-start | bytes 1572872 | tf_op jit(solution)/shard_map/ppermute | solution.py:41
  37.8 4.3 %collective-permute-start.9 = (bf16[128,2048]{1,0:T(8,128)(2,1)S(1)}, bf16[128,2048]{1,0:T(8,128)(2,1)S(1)}, u32[]{:S(2)}, u32[]{:S(2)}) collective-permute-start(bf16[128,2048]{1,0:T(8,128)(2,1)S(1)} %collective-permute-done.2), channel_id=1, source_target_pairs={{0,1},{1,0},{2,3},{3,2},{4,5},{5,4},{6,7},{7,6},{8,9},{9,8},{10,11... | collective-permute-start | bytes 1572872 | tf_op jit(solution)/shard_map/ppermute | solution.py:41
  40.0 2.1 %collective-permute-start.8 = (bf16[128,2048]{1,0:T(8,128)(2,1)S(1)}, bf16[128,2048]{1,0:T(8,128)(2,1)S(1)}, u32[]{:S(2)}, u32[]{:S(2)}) collective-permute-start(bf16[128,2048]{1,0:T(8,128)(2,1)S(1)} %collective-permute-done), channel_id=1, source_target_pairs={{0,1},{1,0},{2,3},{3,2},{4,5},{5,4},{6,7},{7,6},{8,9},{9,8},{10,11... | collective-permute-start | bytes 1572872 | tf_op jit(solution)/shard_map/ppermute | solution.py:41
  43.6 37.0 %collective-permute-start.10 = (f32[128,1024]{1,0:T(8,128)S(1)}, f32[128,1024]{1,0:T(8,128)S(1)}, u32[]{:S(2)}, u32[]{:S(2)}) collective-permute-start(f32[128,1024]{1,0:T(8,128)S(1)} %get-tuple-element.16), channel_id=1, source_target_pairs={{0,16},{8,24},{16,0},{24,8},{1,17},{9,25},{17,1},{25,9},{2,18},{10... | collective-permute-start | bytes 1572872 | tf_op jit(solution)/shard_map/ppermute | solution.py:33
  43.9 25.8 %collective-permute-start.11 = (f32[128,1024]{1,0:T(8,128)S(1)}, f32[128,1024]{1,0:T(8,128)S(1)}, u32[]{:S(2)}, u32[]{:S(2)}) collective-permute-start(f32[128,1024]{1,0:T(8,128)S(1)} %get-tuple-element.17), channel_id=1, source_target_pairs={{0,16},{8,24},{16,0},{24,8},{1,17},{9,25},{17,1},{25,9},{2,18},{10... | collective-permute-start | bytes 1572872 | tf_op jit(solution)/shard_map/ppermute | solution.py:33
  59.0 21.4 %collective-permute-start.5 = (f32[128,1024]{1,0:T(8,128)S(1)}, f32[128,1024]{1,0:T(8,128)S(1)}, u32[]{:S(2)}, u32[]{:S(2)}) collective-permute-start(f32[128,1024]{1,0:T(8,128)S(1)} %slice_add_fusion.8), channel_id=1, source_target_pairs={{0,16},{8,24},{16,0},{24,8},{1,17},{9,25},{17,1},{25,9},{2,18},{10... | collective-permute-start | bytes 1572872 | tf_op jit(solution)/shard_map/ppermute | solution.py:33
  69.7 13.1 %collective-permute-start.12 = (f32[128,1024]{1,0:T(8,128)S(1)}, f32[128,1024]{1,0:T(8,128)S(1)}, u32[]{:S(2)}, u32[]{:S(2)}) collective-permute-start(f32[128,1024]{1,0:T(8,128)S(1)} %slice_add_fusion.6), channel_id=1, source_target_pairs={{0,8},{8,0},{16,24},{24,16},{1,9},{9,1},{17,25},{25,17},{2,10},{10... | collective-permute-start | bytes 1572872 | tf_op jit(solution)/shard_map/ppermute | solution.py:33
  84.8 4.7 %collective-permute-start.15 = (f32[3,2,128]{2,1,0:T(2,128)S(1)}, f32[3,2,128]{2,1,0:T(2,128)S(1)}, u32[]{:S(2)}, u32[]{:S(2)}) collective-permute-start(f32[3,2,128]{2,1,0:T(2,128)S(1)} %pad_maximum_fusion.7), channel_id=1, source_target_pairs={{4,0},{6,2},{0,4},{2,6},{5,1},{7,3},{1,5},{3,7},{12,8},{14,10},{8,... | collective-permute-start | bytes 9224 | tf_op jit(solution)/shard_map/ppermute | solution.py:76
  87.4 3.6 %collective-permute-start.14 = (f32[3,2,128]{2,1,0:T(2,128)S(1)}, f32[3,2,128]{2,1,0:T(2,128)S(1)}, u32[]{:S(2)}, u32[]{:S(2)}) collective-permute-start(f32[3,2,128]{2,1,0:T(2,128)S(1)} %pad_maximum_fusion.7), channel_id=1, source_target_pairs={{2,0},{4,2},{6,4},{0,6},{3,1},{5,3},{7,5},{1,7},{10,8},{12,10},{14... | collective-permute-start | bytes 9224 | tf_op jit(solution)/shard_map/ppermute | solution.py:76
  88.8 5.4 %collective-permute-start.16 = (f32[3,2,128]{2,1,0:T(2,128)S(1)}, f32[3,2,128]{2,1,0:T(2,128)S(1)}, u32[]{:S(2)}, u32[]{:S(2)}) collective-permute-start(f32[3,2,128]{2,1,0:T(2,128)S(1)} %pad_maximum_fusion.7), channel_id=1, source_target_pairs={{6,0},{0,2},{2,4},{4,6},{7,1},{1,3},{3,5},{5,7},{14,8},{8,10},{10,... | collective-permute-start | bytes 9224 | tf_op jit(solution)/shard_map/ppermute | solution.py:76
  94.8 9.2 %collective-permute-start.21 = (bf16[128,1024]{1,0:T(8,128)(2,1)S(1)}, bf16[128,1024]{1,0:T(8,128)(2,1)S(1)}, u32[]{:S(2)}, u32[]{:S(2)}) collective-permute-start(bf16[128,1024]{1,0:T(8,128)(2,1)S(1)} %get-tuple-element.20), channel_id=1, source_target_pairs={{0,16},{8,24},{16,0},{24,8},{1,17},{9,25},{17,1},{25,9},{2,18},{10... | collective-permute-start | bytes 786440 | tf_op jit(solution)/shard_map/ppermute | solution.py:33
  96.2 13.5 %collective-permute-start.18 = (bf16[128,1024]{1,0:T(8,128)(2,1)S(1)}, bf16[128,1024]{1,0:T(8,128)(2,1)S(1)}, u32[]{:S(2)}, u32[]{:S(2)}) collective-permute-start(bf16[128,1024]{1,0:T(8,128)(2,1)S(1)} %get-tuple-element.19), channel_id=1, source_target_pairs={{0,16},{8,24},{16,0},{24,8},{1,17},{9,25},{17,1},{25,9},{2,18},{10... | collective-permute-start | bytes 786440 | tf_op jit(solution)/shard_map/ppermute | solution.py:33
  97.8 9.2 %collective-permute-start.17 = (bf16[128,1024]{1,0:T(8,128)(2,1)S(1)}, bf16[128,1024]{1,0:T(8,128)(2,1)S(1)}, u32[]{:S(2)}, u32[]{:S(2)}) collective-permute-start(bf16[128,1024]{1,0:T(8,128)(2,1)S(1)} %get-tuple-element.19), channel_id=1, source_target_pairs={{0,8},{8,0},{16,24},{24,16},{1,9},{9,1},{17,25},{25,17},{2,10},{10... | collective-permute-start | bytes 786440 | tf_op jit(solution)/shard_map/ppermute | solution.py:33
  99.2 13.1 %collective-permute-start.20 = (bf16[128,1024]{1,0:T(8,128)(2,1)S(1)}, bf16[128,1024]{1,0:T(8,128)(2,1)S(1)}, u32[]{:S(2)}, u32[]{:S(2)}) collective-permute-start(bf16[128,1024]{1,0:T(8,128)(2,1)S(1)} %get-tuple-element.20), channel_id=1, source_target_pairs={{0,8},{8,0},{16,24},{24,16},{1,9},{9,1},{17,25},{25,17},{2,10},{10... | collective-permute-start | bytes 786440 | tf_op jit(solution)/shard_map/ppermute | solution.py:33
  104.1 11.0 %collective-permute-start.22 = (bf16[128,1024]{1,0:T(8,128)(2,1)S(1)}, bf16[128,1024]{1,0:T(8,128)(2,1)S(1)}, u32[]{:S(2)}, u32[]{:S(2)}) collective-permute-start(bf16[128,1024]{1,0:T(8,128)(2,1)S(1)} %collective-permute-done.21), channel_id=1, source_target_pairs={{0,8},{8,0},{16,24},{24,16},{1,9},{9,1},{17,25},{25,17},{2,10},{10... | collective-permute-start | bytes 786440 | tf_op jit(solution)/shard_map/ppermute | solution.py:33
  106.9 17.7 %collective-permute-start.19 = (bf16[128,1024]{1,0:T(8,128)(2,1)S(1)}, bf16[128,1024]{1,0:T(8,128)(2,1)S(1)}, u32[]{:S(2)}, u32[]{:S(2)}) collective-permute-start(bf16[128,1024]{1,0:T(8,128)(2,1)S(1)} %collective-permute-done.17), channel_id=1, source_target_pairs={{0,16},{8,24},{16,0},{24,8},{1,17},{9,25},{17,1},{25,9},{2,18},{10... | collective-permute-start | bytes 786440 | tf_op jit(solution)/shard_map/ppermute | solution.py:33
  122.0 3.0 %collective-permute-start.23 = (f32[128,2048]{1,0:T(8,128)S(1)}, f32[128,2048]{1,0:T(8,128)S(1)}, u32[]{:S(2)}, u32[]{:S(2)}) collective-permute-start(f32[128,2048]{1,0:T(8,128)S(1)} %fusion.41), channel_id=1, source_target_pairs={{0,1},{1,0},{2,3},{3,2},{4,5},{5,4},{6,7},{7,6},{8,9},{9,8},{10,11... | collective-permute-start | bytes 3145736 | tf_op jit(solution)/shard_map/ppermute | solution.py:103
  122.1 10.0 %collective-permute-start.25 = (f32[128,2048]{1,0:T(8,128)S(1)}, f32[128,2048]{1,0:T(8,128)S(1)}, u32[]{:S(2)}, u32[]{:S(2)}) collective-permute-start(f32[128,2048]{1,0:T(8,128)S(1)} %fusion.38), channel_id=1, source_target_pairs={{0,1},{1,0},{2,3},{3,2},{4,5},{5,4},{6,7},{7,6},{8,9},{9,8},{10,11... | collective-permute-start | bytes 3145736 | tf_op jit(solution)/shard_map/ppermute | solution.py:103
  122.6 5.1 %collective-permute-start.27 = (f32[128,2048]{1,0:T(8,128)S(1)}, f32[128,2048]{1,0:T(8,128)S(1)}, u32[]{:S(2)}, u32[]{:S(2)}) collective-permute-start(f32[128,2048]{1,0:T(8,128)S(1)} %fusion.35), channel_id=1, source_target_pairs={{0,1},{1,0},{2,3},{3,2},{4,5},{5,4},{6,7},{7,6},{8,9},{9,8},{10,11... | collective-permute-start | bytes 3145736 | tf_op jit(solution)/shard_map/ppermute | solution.py:103
  124.2 35.2 %collective-permute-start.29 = (f32[128,2048]{1,0:T(8,128)S(1)}, f32[128,2048]{1,0:T(8,128)S(1)}, u32[]{:S(2)}, u32[]{:S(2)}) collective-permute-start(f32[128,2048]{1,0:T(8,128)S(1)} %fusion.32), channel_id=1, source_target_pairs={{0,1},{1,0},{2,3},{3,2},{4,5},{5,4},{6,7},{7,6},{8,9},{9,8},{10,11... | collective-permute-start | bytes 3145736 | tf_op jit(solution)/shard_map/ppermute | solution.py:103
  126.5 11.1 %collective-permute-start.24 = (bf16[128,1024]{1,0:T(8,128)(2,1)S(1)}, bf16[128,1024]{1,0:T(8,128)(2,1)S(1)}, u32[]{:S(2)}, u32[]{:S(2)}) collective-permute-start(bf16[128,1024]{1,0:T(8,128)(2,1)S(1)} %slice.176), channel_id=1, source_target_pairs={{0,2},{2,4},{4,6},{6,0},{1,3},{3,5},{5,7},{7,1},{8,10},{10,12},{12... | collective-permute-start | bytes 786440 | tf_op jit(solution)/shard_map/ppermute | solution.py:116
  129.3 13.1 %collective-permute-start.30 = (bf16[128,1024]{1,0:T(8,128)(2,1)S(1)}, bf16[128,1024]{1,0:T(8,128)(2,1)S(1)}, u32[]{:S(2)}, u32[]{:S(2)}) collective-permute-start(bf16[128,1024]{1,0:T(8,128)(2,1)S(1)} %slice.175), channel_id=1, source_target_pairs={{0,6},{2,0},{4,2},{6,4},{1,7},{3,1},{5,3},{7,5},{8,14},{10,8},{12,... | collective-permute-start | bytes 786440 | tf_op jit(solution)/shard_map/ppermute | solution.py:117
  142.6 11.1 %collective-permute-start.26 = (bf16[128,1024]{1,0:T(8,128)(2,1)S(1)}, bf16[128,1024]{1,0:T(8,128)(2,1)S(1)}, u32[]{:S(2)}, u32[]{:S(2)}) collective-permute-start(bf16[128,1024]{1,0:T(8,128)(2,1)S(1)} %get-tuple-element.12), channel_id=1, source_target_pairs={{0,2},{2,4},{4,6},{6,0},{1,3},{3,5},{5,7},{7,1},{8,10},{10,12},{12... | collective-permute-start | bytes 786440 | tf_op jit(solution)/shard_map/ppermute | solution.py:116
  142.6 13.9 %collective-permute-start.31 = (bf16[128,1024]{1,0:T(8,128)(2,1)S(1)}, bf16[128,1024]{1,0:T(8,128)(2,1)S(1)}, u32[]{:S(2)}, u32[]{:S(2)}) collective-permute-start(bf16[128,1024]{1,0:T(8,128)(2,1)S(1)} %get-tuple-element.13), channel_id=1, source_target_pairs={{0,6},{2,0},{4,2},{6,4},{1,7},{3,1},{5,3},{7,5},{8,14},{10,8},{12,... | collective-permute-start | bytes 786440 | tf_op jit(solution)/shard_map/ppermute | solution.py:117
  153.7 11.2 %collective-permute-start.28 = (bf16[128,1024]{1,0:T(8,128)(2,1)S(1)}, bf16[128,1024]{1,0:T(8,128)(2,1)S(1)}, u32[]{:S(2)}, u32[]{:S(2)}) collective-permute-start(bf16[128,1024]{1,0:T(8,128)(2,1)S(1)} %fusion.25), channel_id=1, source_target_pairs={{0,2},{2,4},{4,6},{6,0},{1,3},{3,5},{5,7},{7,1},{8,10},{10,12},{12... | collective-permute-start | bytes 786440 | tf_op jit(solution)/shard_map/ppermute | solution.py:116
  156.6 12.5 %collective-permute-start.32 = (bf16[128,1024]{1,0:T(8,128)(2,1)S(1)}, bf16[128,1024]{1,0:T(8,128)(2,1)S(1)}, u32[]{:S(2)}, u32[]{:S(2)}) collective-permute-start(bf16[128,1024]{1,0:T(8,128)(2,1)S(1)} %fusion.22), channel_id=1, source_target_pairs={{0,6},{2,0},{4,2},{6,4},{1,7},{3,1},{5,3},{7,5},{8,14},{10,8},{12,... | collective-permute-start | bytes 786440 | tf_op jit(solution)/shard_map/ppermute | solution.py:117
  (7 other events, 58.8 us)
